TPU v7x, 512 devices: a whole 4x8x8 slice. The times are simulated.
512 devices in a mesh: seq: 128 (over y, z, core), head: 4 (over x).
Axes of the slice: x: 4, y: 8, z: 8, core: 2. Of those that a mesh axis runs over, the one named last changes fastest.
Arguments:
- queries: bfloat16 [16384, 1536], P('seq', 'head'), may hold values from -400 to 400
- latent: bfloat16 [16384, 320], P(('seq', 'head')), may hold values from -6 to 6
- w_kv_up: bfloat16 [256, 2048], P(None, 'head'), may hold values from -0.375 to 0.375
Outputs:
- attended: bfloat16 [16384, 1024], P('seq', 'head')
All inputs are finite; a program needn't handle non-finite values.
Results may differ from a plain program's by a relative error of at most 0.004.
Values may be sent and summed in bfloat16 or wider, within the bound.
A program may use at most 64 MiB of HBM per device.

v0:
```python
import math

import jax
import jax.numpy as jnp
from jax import lax
from jax.sharding import PartitionSpec as P

D_LATENT = 256
ROPE = 64
NOPE = 128
VDIM = 128


MASKED = -1e30


def from_everyone(shard, axis):
    copies = jnp.broadcast_to(shard, (lax.axis_size(axis), *shard.shape))
    return lax.all_to_all(copies, axis, split_axis=0, concat_axis=0, tiled=True)


def joined_along(tiles, dim):
    tiles = jnp.moveaxis(tiles, 0, dim)
    dims = tiles.shape
    return tiles.reshape(*dims[:dim], dims[dim] * dims[dim + 1], *dims[dim + 2 :])


def gathered_copies(shard, axis, dim):
    tiles = from_everyone(shard, axis)
    return joined_along(tiles, dim)


def attend(state, key_block, key_start, setup):
    query_side, query_rope, query_pos, w_kv_up, absorb = setup
    numerator, running_max, totals = state
    key_count = key_block.shape[0]
    highest = lax.Precision.HIGHEST
    key_latent = key_block[:, :D_LATENT]
    key_rope = key_block[:, D_LATENT:]
    scores = jnp.einsum(
        "qhd,kd->hqk", query_side, key_latent.astype(jnp.float32), precision=highest
    )
    scores = scores + jnp.einsum(
        "qhd,kd->hqk", query_rope, key_rope, preferred_element_type=jnp.float32
    )
    scores = scores * (NOPE + ROPE) ** (-0.5)
    key_pos = key_start + lax.iota(jnp.int32, key_count)
    allowed = (key_pos[None, :] <= query_pos[:, None]) & (key_pos[None, :] >= 0)
    scores = jnp.where(allowed[None], scores, MASKED)
    new_max = jnp.maximum(running_max, jnp.max(scores, axis=2))
    factor = jnp.exp(running_max - new_max)
    weights = jnp.where(allowed[None], jnp.exp(scores - new_max[:, :, None]), 0.0)
    totals = totals * factor + jnp.sum(weights, axis=2)
    rounded = weights.astype(jnp.bfloat16)
    update = jnp.einsum("hqk,kd->hqd", rounded, key_latent, preferred_element_type=jnp.float32)
    numerator = numerator * factor[:, :, None] + update
    return (numerator, new_max, totals)


def attend_blocks(state, keys, setup):
    key_total = keys.shape[0]
    block_rows = math.gcd(key_total, 1024)
    block_count = key_total // block_rows

    def one_block(block_index, inner):
        offset = block_index * block_rows
        piece = lax.dynamic_slice_in_dim(keys, offset, block_rows, 0)
        return attend(inner, piece, offset, setup)

    return lax.fori_loop(0, block_count, one_block, state)


def prepare(query_rows, query_pos, w_kv_up):
    row_count = query_rows.shape[0]
    local_heads = w_kv_up.shape[1] // (NOPE + VDIM)
    query_all = query_rows.reshape(row_count, local_heads, NOPE + ROPE)
    w_key = w_kv_up.reshape(D_LATENT, local_heads, NOPE + VDIM)[:, :, :NOPE]
    query_side = jnp.einsum(
        "qhn,dhn->qhd", query_all[:, :, :NOPE], w_key, preferred_element_type=jnp.float32
    )
    width = D_LATENT
    setup = (query_side, query_all[:, :, NOPE:], query_pos, w_kv_up, True)
    start_state = (
        jnp.zeros((local_heads, row_count, width), jnp.float32),
        jnp.full((local_heads, row_count), MASKED, jnp.float32),
        jnp.zeros((local_heads, row_count), jnp.float32),
    )
    return (setup, start_state)


def finish(state, w_kv_up):
    numerator, running_max, totals = state
    local_heads = w_kv_up.shape[1] // (NOPE + VDIM)
    row_count = totals.shape[1]
    w_value = w_kv_up.reshape(D_LATENT, local_heads, NOPE + VDIM)[:, :, NOPE:].astype(jnp.float32)
    numerator = jnp.einsum("hqd,dhv->hqv", numerator, w_value, precision=lax.Precision.HIGHEST)
    result = numerator / totals[:, :, None]
    return (
        jnp.transpose(result, (1, 0, 2)).reshape(row_count, local_heads * VDIM).astype(jnp.bfloat16)
    )


def body(queries, latent, w_kv_up):
    group_rows = queries.shape[0]
    group_index = lax.axis_index("seq")
    query_pos = group_index * group_rows + lax.iota(jnp.int32, group_rows)
    setup, state = prepare(queries, query_pos, w_kv_up)
    gathered = gathered_copies(latent, "head", 0)
    state = attend_blocks(state, lax.all_gather(gathered, "seq", axis=0, tiled=True), setup)
    return finish(state, w_kv_up)


def solution(mesh):
    in_specs = (P("seq", "head"), P(("seq", "head"), None), P(None, "head"))
    out_specs = P("seq", "head")
    return jax.shard_map(body, mesh=mesh, in_specs=in_specs, out_specs=out_specs, check_vma=False)
```

profile of v0, /device:TPU:1, one launch (start us, length us, event | category | flops | bytes accessed | tf_op | source)
XLA Modules:
  0.0 202.9 jit_solution(14311295889934789337)
XLA Ops:
  6.5 0.7 broadcast_in_dim.69
  7.3 9.4 %all_to_all.5 = bf16[4,32,320]{2,1,0:T(8,128)(2,1)} all-to-all(bf16[4,32,320]{2,1,0:T(8,128)(2,1)S(1)} %broadcast_in_dim.69), channel_id=1, replica_groups=mesh['seq'=128,'head'=4] {'head'}, dimensions={0} | all-to-all | bytes 163840 | tf_op jit(solution)/shard_map/all_to_all | solution.py:19
  16.7 1.0 copy.14
  17.8 1.1 copy.12
  19.2 93.8 %all-gather.2.cloned.1.call-done = bf16[16384,320]{1,0:T(8,128)(2,1)} async-done(((bf16[128,320]{1,0:T(8,128)(2,1)}), bf16[16384,320]{1,0:T(8,128)(2,1)}) %all-gather.2.cloned.1.call-update) | async-done | bytes 10485776 | tf_op jit(solution)/shard_map/all_gather | solution.py:109
  113.0 82.0 %while.18 = (s32[]{:T(128)}, f32[2,128,256]{2,1,0:T(8,128)S(1)}, f32[2,128]{1,0:T(2,128)S(1)}, f32[2,128]{1,0:T(2,128)S(1)}, bf16[16384,320]{1,0:T(8,128)(2,1)},...) while((s32[]{:T(128)}, f32[2,128,256]{2,1,0:T(8,128)S(1)}, ...), condition=%wide.region_3.4_spmd.clone, body=%wide.region_0.3_spmd.clone.sunk | while | flops 976163200 | bytes 7924967 | solution.py:70
  113.0 0.3 compare_and_fusion.2
  113.4 1.2 fusion.37
  114.6 1.7 fusion.38
  116.5 1.5 convolution_add_fusion.3
  118.1 0.3 compare_and_fusion.2
  118.5 1.2 fusion.37
  119.7 1.7 fusion.38
  121.7 1.5 convolution_add_fusion.3
  123.3 0.3 compare_and_fusion.2
  123.6 1.2 fusion.37
  124.8 1.7 fusion.38
  126.8 1.5 convolution_add_fusion.3
  128.4 0.3 compare_and_fusion.2
  128.7 1.2 fusion.37
  130.0 1.7 fusion.38
  131.9 1.5 convolution_add_fusion.3
  133.5 0.3 compare_and_fusion.2
  133.9 1.2 fusion.37
  135.1 1.7 fusion.38
  137.1 1.5 convolution_add_fusion.3
  138.7 0.3 compare_and_fusion.2
  139.0 1.2 fusion.37
  140.2 1.7 fusion.38
  142.2 1.5 convolution_add_fusion.3
  143.8 0.3 compare_and_fusion.2
  144.1 1.2 fusion.37
  145.4 1.7 fusion.38
  147.3 1.5 convolution_add_fusion.3
  148.9 0.3 compare_and_fusion.2
  149.2 1.2 fusion.37
  150.5 1.7 fusion.38
  152.4 1.5 convolution_add_fusion.3
  154.0 0.3 compare_and_fusion.2
  154.4 1.2 fusion.37
  155.6 1.7 fusion.38
  157.6 1.5 convolution_add_fusion.3
  159.5 1.2 fusion.37
  160.7 1.7 fusion.38
  162.7 1.5 convolution_add_fusion.3
  164.6 1.2 fusion.37
  165.9 1.7 fusion.38
  167.8 1.5 convolution_add_fusion.3
  169.8 1.2 fusion.37
  171.0 1.7 fusion.38
  173.0 1.5 convolution_add_fusion.3
  174.9 1.2 fusion.37
  176.1 1.7 fusion.38
  178.1 1.5 convolution_add_fusion.3
  180.0 1.2 fusion.37
  181.2 1.7 fusion.38
  183.2 1.5 convolution_add_fusion.3
  185.2 1.2 fusion.37
  186.4 1.7 fusion.38
  188.3 1.5 convolution_add_fusion.3
  190.3 1.2 fusion.37
  191.5 1.7 fusion.38
  193.5 1.5 convolution_add_fusion.3
  195.3 0.7 copy.17
  (128 shorter events, 7.3 us)
Async XLA Ops:
  6.5 106.5 %all-gather.2.cloned.1.call-start = ((), (), s32[]{:S(2)}) async-start(), calls=%async_computation.1 | async-start | bytes 12681216 | tf_op jit(solution)/shard_map/all_gather | solution.py:109
Sparse Core Ops, SparseCore 0:
  16.8 96.1 all-gather.1
where the time goes:
time: 205 us; the launch traced here: 203 us
  waiting for transfers between devices  93.8 us (46%)
  matrix products  71.6 us (35%)
  between operations  13.5 us (7%)
  other arithmetic  9.62 us (5%)
  blocking collectives  9.39 us (5%)
  local copies, waits for them, and re-layouts  3.76 us (2%)
    all_gather x1, waiting for transfers between devices, body(): lax.all_gather(gathered, 'seq', axis=0, tiled=True)  93.8 us
    dot_general x16, matrix products, attend(): jnp.einsum('qhd,kd->hqk', query_side, key_latent.astype(jnp.float32), pre...  27.3 us
    dot_general x16, matrix products, attend(): jnp.einsum('hqk,kd->hqd', rounded, key_latent, preferred_element_type=jnp...  24.2 us
    dot_general x16, matrix products, attend(): jnp.einsum('qhd,kd->hqk', query_rope, key_rope, preferred_element_type=jn...  19.6 us
    all_to_all x1, blocking collectives, from_everyone(): return lax.all_to_all(copies, axis, split_axis=0, concat_axis=0, tiled=True)  9.39 us
    and x16, other arithmetic, attend(): allowed = (key_pos[None, :] <= query_pos[:, None]) & (key_pos[None, :] >= 0)  5.39 us
  transfers between devices with their start and end apart: 1, of which 1 were waited for; matrix products, arithmetic and copies ran while one was open for 1% of the time, Pallas kernels for 0%

commit v1 on v0

v1 whole, which is shorter than its diff:
```python
import math

import jax
import jax.numpy as jnp
from jax import lax
from jax.experimental import pallas as pl
from jax.experimental.pallas import tpu as pltpu
from jax.sharding import PartitionSpec as P

D_LATENT = 256
ROPE = 64
NOPE = 128
VDIM = 128
QW = NOPE + ROPE
MASKED = -1e30
FLOOR = -1e29
SCALE = QW ** (-0.5) * math.log2(math.e)
F32 = jnp.float32
BF16 = jnp.bfloat16


def two_pieces(value):
    high = value.astype(BF16)
    low = (value - high.astype(F32)).astype(BF16)
    return high, low


def prepare_pair(q_all, w_all, side_ref, row):
    for j in range(2):
        q = q_all[:, j * QW : (j + 1) * QW]
        nope = q[:, :NOPE].astype(BF16)
        rope = q[:, NOPE:] * SCALE
        w_key = w_all[:, j * 256 : j * 256 + 128]
        side = lax.dot_general(nope, w_key, (((1,), (1,)), ((), ())), preferred_element_type=F32)
        high, low = two_pieces(side * SCALE)
        rows = pl.ds(row + j * 128, 128)
        side_ref[rows, 0:256] = high
        side_ref[rows, 256:512] = low
        rope_high, rope_low = two_pieces(rope)
        side_ref[rows, 512:640] = jnp.concatenate([rope_high, rope_low], axis=1)


def flash_rows(side_ref, key, key_t, allowed, m_ref, l_ref, acc_ref, row, count):
    rows = pl.ds(row, count)
    scores = jnp.dot(side_ref[rows, :], key_t, preferred_element_type=F32)
    if allowed is not None:
        scores = jnp.where(allowed, scores, MASKED)
    old_max = m_ref[rows, :]
    new_max = jnp.maximum(old_max, jnp.max(scores, axis=1, keepdims=True))
    factor = jnp.exp2(old_max - new_max)
    weights = jnp.exp2(scores - new_max[:, :1])
    lanes = weights[:, 0:128]
    for piece in range(1, weights.shape[1] // 128):
        lanes = lanes + weights[:, piece * 128 : (piece + 1) * 128]
    l_ref[rows, :] = l_ref[rows, :] * factor + lanes
    update = jnp.dot(weights.astype(BF16), key, preferred_element_type=F32)
    acc_ref[rows, :] = acc_ref[rows, :] * jnp.concatenate([factor, factor], axis=1) + update
    m_ref[rows, :] = new_max


def finish_head(w_all, m_ref, l_ref, acc_ref, row, j):
    rows = pl.ds(row + j * 128, 128)
    total = jnp.sum(l_ref[rows, :], axis=1, keepdims=True)
    normal = acc_ref[rows, :] / jnp.maximum(total, 1.0)
    high, low = two_pieces(normal)
    w_value = w_all[:, j * 256 + 128 : j * 256 + 256]
    out = jnp.dot(high, w_value, preferred_element_type=F32)
    out = out + jnp.dot(low, w_value, preferred_element_type=F32)
    m_row = m_ref[rows, :].T[0:1, :]
    l_row = jnp.broadcast_to(total, (128, 128)).T[0:1, :]
    return out, m_row, l_row


CHUNK = 256


def kernel(q_ref, w_ref, k_ref, o_ref, st_ref, side_ref, m_ref, l_ref, acc_ref, kt_ref):
    group = lax.axis_index("seq")
    part = lax.axis_index("head")
    m_ref[...] = jnp.full_like(m_ref, FLOOR)
    l_ref[...] = jnp.zeros_like(l_ref)
    acc_ref[...] = jnp.zeros_like(acc_ref)
    for p in range(4):
        prepare_pair(q_ref[p].astype(F32), w_ref[p], side_ref, p * 256)

    def one_chunk(c, carry):
        key = k_ref[pl.ds(c * CHUNK, CHUNK), 0:256]
        rope = k_ref[pl.ds(c * CHUNK, CHUNK), 256:320]
        key_t = key.T
        rope_t = rope.T
        kt_ref[0:256, :] = key_t
        kt_ref[256:512, :] = key_t
        kt_ref[512:576, :] = rope_t
        kt_ref[576:640, :] = rope_t
        col = lax.broadcasted_iota(jnp.int32, (1, CHUNK), 1)
        key_pos = (c * (CHUNK // 32) + col // 32) * 128 + part * 32 + col % 32
        query_pos = group * 128 + lax.broadcasted_iota(jnp.int32, (128, 1), 0)
        allowed = key_pos <= query_pos
        allowed = jnp.concatenate([allowed, allowed], axis=0)
        for p in range(4):
            flash_rows(side_ref, key, kt_ref[...], allowed, m_ref, l_ref, acc_ref, p * 256, 256)
        return carry

    lax.fori_loop(0, group * 32 // CHUNK + 1, one_chunk, 0)
    for p in range(4):
        st_ref[p] = jnp.zeros((8, 128), F32)
        for j in range(2):
            out, m_row, l_row = finish_head(w_ref[p], m_ref, l_ref, acc_ref, p * 256, j)
            o_ref[p, :, j * 128 : (j + 1) * 128] = out
            st_ref[p, 2 * j : 2 * j + 1, :] = m_row
            st_ref[p, 2 * j + 1 : 2 * j + 2, :] = l_row


def body(queries, latent, w_kv_up):
    keys = lax.all_gather(latent, "seq", axis=0, tiled=True)
    q_all = lax.all_gather(queries, "head", axis=0)
    w_all = lax.all_gather(w_kv_up, "head", axis=0)
    out, stats = pl.pallas_call(
        kernel,
        out_shape=[
            jax.ShapeDtypeStruct((4, 128, 256), F32),
            jax.ShapeDtypeStruct((4, 8, 128), F32),
        ],
        in_specs=[pl.BlockSpec(memory_space=pltpu.VMEM)] * 3,
        out_specs=[pl.BlockSpec(memory_space=pltpu.VMEM)] * 2,
        scratch_shapes=[
            pltpu.VMEM((1024, 640), BF16),
            pltpu.VMEM((1024, 128), F32),
            pltpu.VMEM((1024, 128), F32),
            pltpu.VMEM((1024, 256), F32),
            pltpu.VMEM((640, CHUNK), BF16),
        ],
        compiler_params=pltpu.CompilerParams(vmem_limit_bytes=40 * 1024 * 1024),
    )(q_all, w_all, keys)
    out = lax.all_to_all(out, "head", 0, 0, tiled=True)
    stats = lax.all_to_all(stats, "head", 0, 0, tiled=True)
    heads = []
    for j in range(2):
        m = stats[:, 2 * j]
        total = stats[:, 2 * j + 1]
        weight = jnp.exp2(m - jnp.max(m, axis=0, keepdims=True)) * total
        weight = weight / jnp.sum(weight, axis=0, keepdims=True)
        heads.append(jnp.sum(out[:, :, j * 128 : (j + 1) * 128] * weight[:, :, None], axis=0))
    return jnp.concatenate(heads, axis=1).astype(BF16)


def solution(mesh):
    in_specs = (P("seq", "head"), P(("seq", "head"), None), P(None, "head"))
    out_specs = P("seq", "head")
    return jax.shard_map(body, mesh=mesh, in_specs=in_specs, out_specs=out_specs, check_vma=False)
```

time: 205 us -> 198 us (0.966)
  the two profiles are of different devices: /device:TPU:1 before, /device:TPU:56 now
where the time goes in v1:
time: 198 us
  waiting for transfers between devices  118 us (60%)
  Pallas kernels  36.6 us (18%)
  blocking collectives  22.5 us (11%)
  between operations  13.4 us (7%)
  starting transfers between devices  3.51 us (2%)
  local copies, waits for them, and re-layouts  3.12 us (2%)
    all_gather x1, waiting for transfers between devices, body(): keys = lax.all_gather(latent, 'seq', axis=0, tiled=True)  86.2 us
    pallas_call x1, Pallas kernels, body(): pl.pallas_call(kernel, out_shape=[jax.ShapeDtypeStruct((4, 128, 256), F32...  36.6 us
    all_gather x1, waiting for transfers between devices, body(): w_all = lax.all_gather(w_kv_up, 'head', axis=0)  21.8 us
    all_gather x1, blocking collectives, body(): q_all = lax.all_gather(queries, 'head', axis=0)  13.1 us
    all_to_all x1, blocking collectives, body(): stats = lax.all_to_all(stats, 'head', 0, 0, tiled=True)  9.4 us
    all_to_all x1, waiting for transfers between devices, body(): out = lax.all_to_all(out, 'head', 0, 0, tiled=True)  8.57 us
  transfers between devices with their start and end apart: 3, of which 3 were waited for; matrix products, arithmetic and copies ran while one was open for 0% of the time, Pallas kernels for 0%

profile of v1, /device:TPU:56, one launch (start us, length us, event | category | flops | bytes accessed | tf_op | source)
XLA Modules:
  0.0 198.1 jit_solution(3776493431948586130)
XLA Ops:
  6.5 0.0 all-gather.7.cloned.1.call-start
  6.5 0.7 all-gather.7.cloned.1.call-update
  7.3 0.0 all-gather.5.cloned.1.call-start
  7.3 0.7 all-gather.5.cloned.1.call-update
  8.0 13.1 %all-gather = bf16[512,384]{1,0:T(8,128)(2,1)S(1)} all-gather(bf16[128,384]{1,0:T(8,128)(2,1)} %param.3), channel_id=2, replica_groups=mesh['seq'=128,'head'=4] {'head'}, dimensions={0}, use_global_device_ids=true | all-gather | bytes 491520 | tf_op jit(solution)/shard_map/all_gather | solution.py:116
  21.1 21.8 %all-gather.7.cloned.1.call-done = bf16[1024,512]{1,0:T(8,128)(2,1)} async-done(((bf16[256,512]{1,0:T(8,128)(2,1)}), bf16[1024,512]{1,0:T(8,128)(2,1)}) %all-gather.7.cloned.1.call-update) | async-done | bytes 1048592 | tf_op jit(solution)/shard_map/all_gather | solution.py:117
  42.9 86.2 %all-gather.5.cloned.1.call-done.k_ref = bf16[4096,320]{1,0:T(8,128)(2,1)} async-done(((bf16[32,320]{1,0:T(8,128)(2,1)}), bf16[4096,320]{1,0:T(8,128)(2,1)}) %all-gather.5.cloned.1.call-update) | async-done | bytes 2621456 | tf_op jit(solution)/shard_map/all_gather | solution.py:115
  129.1 0.0 copy-start
  129.2 1.9 copy-done
  131.0 0.0 copy-start.1
  131.0 1.2 copy-done.1
  132.3 36.6 %shard_map.37 = (f32[4,128,256]{2,1,0:T(8,128)}, f32[4,8,128]{2,1,0:T(8,128)S(1)}) custom-call(bf16[4,128,384]{2,1,0:T(8,128)(2,1)S(1)} %bitcast.12, bf16[4,256,512]{2,1,0:T(8,128)(2,1)S(1)} %bitcast.13, bf16[4096,320]{1,0:T(8,128)(2,1)S(1)} %copy-done), custom_call_target="tpu_custom_call" | custom-call | tf_op jit(solution)/shard_map/pallas_call | solution.py:118
  168.9 9.4 %all_to_all.10 = f32[4,8,128]{2,1,0:T(8,128)S(1)} all-to-all(f32[4,8,128]{2,1,0:T(8,128)S(1)} %get-tuple-element.8), channel_id=1, replica_groups=mesh['seq'=128,'head'=4] {'head'}, dimensions={0} | all-to-all | bytes 32768 | tf_op jit(solution)/shard_map/all_to_all | solution.py:136
  178.3 3.5 %all-to-all-start = ((f32[4,128,256]{2,1,0:T(8,128)}), f32[4,128,256]{2,1,0:T(8,128)S(1)}, u32[]{:S(2)}, u32[]{:S(2)}) async-start(f32[4,128,256]{2,1,0:T(8,128)} %get-tuple-element.7), calls=%async_computation | async-start | bytes 1048576 | tf_op jit(solution)/shard_map/all_to_all | solution.py:135
  181.9 8.6 %all-to-all-done = f32[4,128,256]{2,1,0:T(8,128)S(1)} async-done(((f32[4,128,256]{2,1,0:T(8,128)}), f32[4,128,256]{2,1,0:T(8,128)S(1)}, u32[]{:S(2)}, u32[]{:S(2)}) %all-to-all-start) | async-done | bytes 524320 | tf_op jit(solution)/shard_map/all_to_all | solution.py:135
  190.4 0.2 fusion.1
  190.6 0.6 pad_maximum_fusion
  (6 shorter events, 0.1 us)
Async XLA Ops:
  6.5 36.4 %all-gather.7.cloned.1.call-start = ((), (), s32[]{:S(2)}) async-start(), calls=%async_computation.3 | async-start | bytes 1310720 | tf_op jit(solution)/shard_map/all_gather | solution.py:117
  7.3 121.9 %all-gather.5.cloned.1.call-start = ((), (), s32[]{:S(2)}) async-start(), calls=%async_computation.2 | async-start | bytes 3170304 | tf_op jit(solution)/shard_map/all_gather | solution.py:115
  129.1 1.9 copy-start
  131.0 1.2 copy-start.1
  178.3 12.2 %all-to-all-start = ((f32[4,128,256]{2,1,0:T(8,128)}), f32[4,128,256]{2,1,0:T(8,128)S(1)}, u32[]{:S(2)}, u32[]{:S(2)}) async-start(f32[4,128,256]{2,1,0:T(8,128)} %get-tuple-element.7), calls=%async_computation | async-start | bytes 1048576 | tf_op jit(solution)/shard_map/all_to_all | solution.py:135
Sparse Core Ops, SparseCore 0:
  9.4 33.4 all-gather.6
  46.0 83.0 all-gather.4

commit v2 on v1

v2 whole, which is shorter than its diff:
```python
import math

import jax
import jax.numpy as jnp
from jax import lax
from jax.experimental import pallas as pl
from jax.experimental.pallas import tpu as pltpu
from jax.sharding import PartitionSpec as P

D_LATENT = 256
ROPE = 64
NOPE = 128
VDIM = 128
QW = NOPE + ROPE
MASKED = -1e30
FLOOR = -1e29
SCALE = QW ** (-0.5) * math.log2(math.e)
F32 = jnp.float32
BF16 = jnp.bfloat16
MESH = pl.DeviceIdType.MESH
CH = 256
OFFSETS = (0, 1, 7, 2, 6, 3, 5, 4)


def two_pieces(value):
    high = value.astype(BF16)
    low = (value - high.astype(F32)).astype(BF16)
    return high, low


def prepare_pair(q_ref, w_ref, side_ref, p):
    q = q_ref[p].astype(F32)
    rope = (q[:, 128:256].T[0:64], q[:, 256:384].T[64:128])
    for j in range(2):
        nope = q[:, j * QW : j * QW + NOPE].astype(BF16)
        side = lax.dot_general(
            w_ref[p, 2 * j], nope, (((1,), (1,)), ((), ())), preferred_element_type=F32
        )
        high, low = two_pieces(side * SCALE)
        rope_high, rope_low = two_pieces(rope[j] * SCALE)
        columns = slice(j * 128, (j + 1) * 128)
        side_ref[p, 0:256, columns] = high
        side_ref[p, 256:512, columns] = low
        side_ref[p, 512:640, columns] = jnp.concatenate([rope_high, rope_low], axis=0)


def load_chunk(k_ref, c, lhs_ref, kt_ref):
    key = k_ref[c, :, 0:256]
    rope = k_ref[c, :, 256:320]
    lhs_ref[:, 0:256] = key
    lhs_ref[:, 256:384] = jnp.concatenate([rope, rope], axis=1)
    kt_ref[...] = key.T


def scores_of(lhs_ref, side_ref, s_ref, p):
    key = lhs_ref[:, 0:256]
    lhs = jnp.concatenate([key, key, lhs_ref[:, 256:384]], axis=1)
    s_ref[p] = jnp.dot(lhs, side_ref[p], preferred_element_type=F32)


def soften(s_ref, kt_ref, bias_ref, st_ref, acc_ref, p):
    bias = bias_ref[...]
    scores = s_ref[p] + jnp.concatenate([bias, bias], axis=1)
    old = st_ref[p, 0:1, :]
    new = jnp.maximum(old, jnp.max(scores, axis=0, keepdims=True))
    factor = jnp.exp2(old - new)
    weights = jnp.exp2(scores - new)
    st_ref[p, 1:2, :] = st_ref[p, 1:2, :] * factor + jnp.sum(weights, axis=0, keepdims=True)
    update = jnp.dot(kt_ref[...], weights.astype(BF16), preferred_element_type=F32)
    acc_ref[p] = acc_ref[p] * factor + update
    st_ref[p, 0:1, :] = new


def finish_pair(w_ref, st_ref, acc_ref, p):
    outs = []
    for j in range(2):
        columns = slice(j * 128, (j + 1) * 128)
        total = jnp.maximum(st_ref[p, 1:2, columns], 1.0)
        high, low = two_pieces(acc_ref[p, :, columns] / total)
        value_t = w_ref[p, 2 * j + 1].T
        out = jnp.dot(value_t, high, preferred_element_type=F32)
        outs.append(out + jnp.dot(value_t, low, preferred_element_type=F32))
    return outs


def kernel(
    q_hbm, lat_hbm, w_hbm, o_ref,
    k_ref, q_ref, w_ref, side_ref, acc_ref, st_ref, base_ref,
    lhs_a, kt_a, s_a, bias_a, lhs_b, kt_b, s_b, bias_b,
    out_ref, gout_ref, gst_ref,
    load_sem, near_send, near_recv, k_recv, ring_send, sib_send,
    x_send, x_recv, w_recv, wsib_send, out_send, out_recv, st_send, st_recv,
):
    seq = lax.axis_index("seq")
    x = lax.axis_index("head")
    core = lax.rem(seq, 2)
    z = lax.rem(lax.div(seq, 2), 8)
    y = lax.div(seq, 16)
    ia = z + core * (y - z)
    ib = y + core * (z - y)

    def at(a, b):
        a = lax.rem(a, 8)
        b = lax.rem(b, 8)
        to_y = b + core * (a - b)
        to_z = a + core * (b - a)
        return ((to_y * 8 + to_z) * 2 + core, x)

    sibling = (seq + 1 - 2 * core, x)
    up = at(ia, ib + 1)
    down = at(ia, ib + 7)

    def peer(e):
        return (seq, lax.rem(x + e, 4))

    def copy(src, dst, send, recv, to):
        return pltpu.make_async_remote_copy(
            src_ref=src, dst_ref=dst, send_sem=send, recv_sem=recv, device_id=to, device_id_type=MESH
        )

    loads = [
        pltpu.make_async_copy(lat_hbm, k_ref.at[0, pl.ds(0, 32)], load_sem.at[0]),
        pltpu.make_async_copy(q_hbm, q_ref.at[0], load_sem.at[1]),
    ]
    for part in range(4):
        loads.append(
            pltpu.make_async_copy(
                w_hbm.at[:, pl.ds(part * 128, 128)], w_ref.at[0, part], load_sem.at[2 + part]
            )
        )
    for load in loads:
        load.start()

    barrier = pltpu.get_barrier_semaphore()
    for e in range(1, 8):
        pl.semaphore_signal(barrier, inc=1, device_id=at(ia + e, ib), device_id_type=MESH)
    for to in (up, down, sibling, peer(1), peer(2), peer(3)):
        pl.semaphore_signal(barrier, inc=1, device_id=to, device_id_type=MESH)

    row = lax.broadcasted_iota(jnp.int32, (CH, 128), 0)
    slot = row // 32
    half = (slot + 1) // 2
    offset = jnp.where(slot % 2 == 1, half, (8 - half) % 8)
    for which in range(2):
        color = core if which == 0 else 1 - core
        start = z + color * (y - z)
        along = (start + offset) % 8
        base_ref[which] = along * (256 + color * 1792) + color * 128 + x * 32 + row % 32

    def set_bias(bias_ref, c):
        hop = lax.div(c + 2, 4)
        late = lax.rem(c + 2, 4)
        edge = jnp.logical_or(c < 2, c > 13)
        which = jnp.where(edge, lax.rem(c, 2), lax.div(late, 2))
        db = jnp.where(c < 2, 0, jnp.where(c > 13, 4, jnp.where(lax.rem(c, 2) == 0, 8 - hop, hop)))
        color = core + which * (1 - 2 * core)
        start = y + color * (z - y)
        moved = lax.rem(start + db, 8) * (2048 - color * 1792)
        query = seq * 128 + lax.broadcasted_iota(jnp.int32, (CH, 128), 1)
        bias_ref[...] = jnp.where(base_ref[which] <= query - moved, 0.0, MASKED)

    for load in loads:
        load.wait()
    pl.semaphore_wait(barrier, 13)

    near = []
    for j in range(1, 8):
        e = (8 - OFFSETS[j]) % 8
        near.append(
            copy(
                k_ref.at[0, pl.ds(0, 32)], k_ref.at[0, pl.ds(j * 32, 32)],
                near_send.at[j], near_recv.at[j], at(ia + e, ib),
            )
        )
    for one in near:
        one.start()
    w_key = []
    w_value = []
    q_copies = []
    for e in (1, 3, 2):
        s = 4 - e
        w_key.append(
            copy(w_ref.at[0, 2 * core], w_ref.at[s, 2 * core], x_send.at[0, e], x_recv.at[0, s], peer(e))
        )
        q_copies.append(copy(q_ref.at[0], q_ref.at[s], x_send.at[1, e], x_recv.at[1, s], peer(e)))
        w_value.append(
            copy(
                w_ref.at[0, 2 * core + 1], w_ref.at[s, 2 * core + 1],
                x_send.at[2, e], x_recv.at[2, s], peer(e),
            )
        )
    for one in w_key + q_copies + w_value:
        one.start()

    st_ref[:, 0:1, :] = jnp.full((4, 1, 256), FLOOR, F32)
    st_ref[:, 1:8, :] = jnp.zeros((4, 7, 256), F32)
    acc_ref[...] = jnp.zeros_like(acc_ref)
    prepare_pair(q_ref, w_ref, side_ref, 0)

    def quarter(c, q):
        return k_ref.at[c, pl.ds(q * 64, 64)]

    def ring(direction, hop, src, dst, q, to):
        return copy(quarter(src, q), quarter(dst, q), ring_send.at[direction, hop, q], k_recv.at[dst, q], to)

    def across(src, dst, q):
        return copy(quarter(src, q), quarter(dst, q), sib_send.at[dst, q], k_recv.at[dst, q], sibling)

    def arrived(c, q):
        copy(quarter(c, q), quarter(c, q), sib_send.at[c, q], k_recv.at[c, q], sibling).wait_recv()

    for q in range(4):
        for j in (2 * q, 2 * q + 1):
            if j > 0:
                near[j - 1].wait_recv()
        ring(0, 0, 0, 2, q, up).start()
        ring(1, 0, 0, 3, q, down).start()
        across(0, 1, q).start()

    def w_across(s, part):
        return copy(
            w_ref.at[s, 2 * core + part], w_ref.at[s, 2 * core + part],
            wsib_send.at[part, s], w_recv.at[part, s], sibling,
        )

    def w_arrived(s, part):
        other = 2 - 2 * core + part
        copy(
            w_ref.at[s, other], w_ref.at[s, other], wsib_send.at[part, s], w_recv.at[part, s], sibling
        ).wait_recv()

    for s in (3, 1, 2):
        copy(w_ref.at[0, 2 * core], w_ref.at[s, 2 * core], x_send.at[0, s], x_recv.at[0, s], peer(s)).wait_recv()
        w_across(s, 0).start()

    for q in range(4):
        arrived(2, q)
        ring(0, 1, 2, 6, q, up).start()
        across(2, 4, q).start()
        arrived(3, q)
        ring(1, 1, 3, 7, q, down).start()
        across(3, 5, q).start()

    for s in (3, 1, 2):
        copy(q_ref.at[0], q_ref.at[s], x_send.at[1, s], x_recv.at[1, s], peer(s)).wait_recv()
        w_arrived(s, 0)
        prepare_pair(q_ref, w_ref, side_ref, s)

    def event(i, part):
        q = 2 * lax.rem(i, 2) + part

        @pl.when(i < 4)
        def _():
            hop = 2 + lax.div(i, 2)
            above = 4 * hop - 2
            below = 4 * hop - 1
            arrived(above, q)

            @pl.when(jnp.logical_or(i < 2, q < 2))
            def _():
                ring(0, hop, above, above + 4, q, up).start()

            across(above, above + 2, q).start()
            arrived(below, q)

            @pl.when(i < 2)
            def _():
                ring(1, hop, below, below + 4, q, down).start()

            @pl.when(i == 3)
            def _():
                ring(1, hop, below, below + 3, q, down).start()

            across(below, below + 2, q).start()

        @pl.when(jnp.logical_and(i >= 4, i < 6))
        def _():
            arrived(14, q)
            across(14, 15, q).start()

    def bundle_arrived(c):
        for q in range(4):
            arrived(c, q)

    first = (lhs_a, kt_a, s_a, bias_a)
    second = (lhs_b, kt_b, s_b, bias_b)

    load_chunk(k_ref, 0, lhs_a, kt_a)
    set_bias(bias_a, 0)
    for p in range(4):
        scores_of(lhs_a, side_ref, s_a, p)

    def half_step(c, now, later):
        load_chunk(k_ref, c + 1, later[0], later[1])
        set_bias(later[3], c + 1)
        for p in range(4):
            scores_of(later[0], side_ref, later[2], p)
            soften(now[2], now[1], now[3], st_ref, acc_ref, p)

    def two_chunks(i, carry):
        event(i, 0)

        @pl.when(jnp.logical_or(lax.rem(i, 2) == 0, i == 7))
        def _():
            bundle_arrived(2 * i + 1)

        half_step(2 * i, first, second)
        event(i, 1)

        @pl.when(jnp.logical_and(lax.rem(i, 2) == 1, i < 7))
        def _():
            bundle_arrived(2 * i + 2)

        @pl.when(i < 7)
        def _():
            half_step(2 * i + 1, second, first)

        return carry

    lax.fori_loop(0, 8, two_chunks, 0)
    for p in range(4):
        soften(s_b, kt_b, bias_b, st_ref, acc_ref, p)

    for s in (3, 1, 2):
        copy(
            w_ref.at[0, 2 * core + 1], w_ref.at[s, 2 * core + 1], x_send.at[2, s], x_recv.at[2, s], peer(s)
        ).wait_recv()
        w_across(s, 1).start()

    def send_out(e):
        s = 4 - e
        copy(st_ref.at[e], gst_ref.at[s], st_send.at[e], st_recv.at[s], peer(e)).start()
        copy(out_ref.at[e], gout_ref.at[s], out_send.at[e], out_recv.at[s], peer(e)).start()

    order = (2, 1, 3)
    for n, e in enumerate(order):
        w_arrived(e, 1)
        out = finish_pair(w_ref, st_ref, acc_ref, e)
        out_ref[e, 0:128, :] = out[0].astype(BF16)
        out_ref[e, 128:256, :] = out[1].astype(BF16)
        if n > 0:
            send_out(order[n - 1])
    own = finish_pair(w_ref, st_ref, acc_ref, 0)
    send_out(order[2])

    for s in (2, 3, 1):
        copy(st_ref.at[s], gst_ref.at[s], st_send.at[s], st_recv.at[s], peer(s)).wait_recv()
        copy(out_ref.at[s], gout_ref.at[s], out_send.at[s], out_recv.at[s], peer(s)).wait_recv()
    for j in range(2):
        columns = slice(j * 128, (j + 1) * 128)
        tops = [st_ref[0, 0:1, columns]] + [gst_ref[s, 0:1, columns] for s in (1, 2, 3)]
        sums = [st_ref[0, 1:2, columns]] + [gst_ref[s, 1:2, columns] for s in (1, 2, 3)]
        parts = [own[j]] + [gout_ref[s, columns, :].astype(F32) for s in (1, 2, 3)]
        top = jnp.maximum(jnp.maximum(tops[0], tops[1]), jnp.maximum(tops[2], tops[3]))
        shares = [jnp.exp2(tops[s] - top) * sums[s] for s in range(4)]
        whole = shares[0] + shares[1] + shares[2] + shares[3]
        result = parts[0] * (shares[0] / whole)
        for s in range(1, 4):
            result = result + parts[s] * (shares[s] / whole)
        o_ref[:, columns] = result.T.astype(BF16)

    for one in near + w_key + q_copies + w_value:
        one.wait_send()
    for e in (1, 2, 3):
        copy(st_ref.at[e], gst_ref.at[e], st_send.at[e], st_recv.at[e], peer(e)).wait_send()
        copy(out_ref.at[e], gout_ref.at[e], out_send.at[e], out_recv.at[e], peer(e)).wait_send()
        w_across(e, 0).wait_send()
        w_across(e, 1).wait_send()
    for q in range(4):
        for hop in range(3):
            ring(0, hop, 0, 2, q, up).wait_send()
            ring(1, hop, 0, 2, q, down).wait_send()
        ring(0 if q < 2 else 1, 3, 0, 2, q, up).wait_send()
        for c in (1, 4, 5, 8, 9, 12, 13, 15):
            across(0, c, q).wait_send()


def body(queries, latent, w_kv_up):
    dma = pltpu.SemaphoreType.DMA
    chunk = [
        pltpu.VMEM((CH, 384), BF16),
        pltpu.VMEM((256, CH), BF16),
        pltpu.VMEM((4, CH, 256), F32),
        pltpu.VMEM((CH, 128), F32),
    ]
    return pl.pallas_call(
        kernel,
        out_shape=jax.ShapeDtypeStruct((128, 256), BF16),
        in_specs=[pl.BlockSpec(memory_space=pl.ANY)] * 3,
        out_specs=pl.BlockSpec(memory_space=pltpu.VMEM),
        scratch_shapes=[
            pltpu.VMEM((16, CH, 320), BF16),
            pltpu.VMEM((4, 128, 384), BF16),
            pltpu.VMEM((4, 4, 256, 128), BF16),
            pltpu.VMEM((4, 640, 256), BF16),
            pltpu.VMEM((4, 256, 256), F32),
            pltpu.VMEM((4, 8, 256), F32),
            pltpu.VMEM((2, CH, 128), jnp.int32),
            *chunk,
            *chunk,
            pltpu.VMEM((4, 256, 128), BF16),
            pltpu.VMEM((4, 256, 128), BF16),
            pltpu.VMEM((4, 8, 256), F32),
            dma((6,)),
            dma((8,)),
            dma((8,)),
            dma((16, 4)),
            dma((2, 4, 4)),
            dma((16, 4)),
            dma((3, 4)),
            dma((3, 4)),
            dma((2, 4)),
            dma((2, 4)),
            dma((4,)),
            dma((4,)),
            dma((4,)),
            dma((4,)),
        ],
        compiler_params=pltpu.CompilerParams(
            vmem_limit_bytes=40 * 1024 * 1024, collective_id=0, has_side_effects=True
        ),
    )(queries, latent, w_kv_up)


def solution(mesh):
    in_specs = (P("seq", "head"), P(("seq", "head"), None), P(None, "head"))
    out_specs = P("seq", "head")
    return jax.shard_map(body, mesh=mesh, in_specs=in_specs, out_specs=out_specs, check_vma=False)
```

time: 198 us -> 53.6 us (0.27)
  the two profiles are of different devices: /device:TPU:56 before, /device:TPU:1 now
where the time goes in v2:
time: 53.6 us; the launch traced here: 53.3 us
  Pallas kernels  50.1 us (93%)
  local copies, waits for them, and re-layouts  3.21 us (6%)
    pallas_call x1, Pallas kernels, body(): pl.pallas_call(kernel, out_shape=jax.ShapeDtypeStruct((128, 256), BF16),...  50.1 us
    unnamed x7, local copies, waits for them, and re-layouts  3.21 us

profile of v2, /device:TPU:1, one launch (start us, length us, event | category | flops | bytes accessed | tf_op | source)
XLA Modules:
  0.0 53.3 jit_solution(16797008229145087185)
XLA Ops:
  0.0 0.0 copy-start
  0.0 0.9 %copy-done = bf16[256,512]{1,0:T(8,128)(2,1)S(1)} copy-done((bf16[256,512]{1,0:T(8,128)(2,1)S(1)}, bf16[256,512]{1,0:T(8,128)(2,1)}, u32[]{:S(2)}) %copy-start) | copy-done | bytes 262168
  1.0 0.0 copy-start.1
  1.0 0.9 %copy-done.1 = bf16[128,384]{1,0:T(8,128)(2,1)S(1)} copy-done((bf16[128,384]{1,0:T(8,128)(2,1)S(1)}, bf16[128,384]{1,0:T(8,128)(2,1)}, u32[]{:S(2)}) %copy-start.1) | copy-done | bytes 98328
  1.8 0.0 copy-start.2
  1.8 0.7 %copy-done.2 = bf16[32,320]{1,0:T(8,128)(2,1)S(1)} copy-done((bf16[32,320]{1,0:T(8,128)(2,1)S(1)}, bf16[32,320]{1,0:T(8,128)(2,1)}, u32[]{:S(2)}) %copy-start.2) | copy-done | bytes 20504
  2.6 50.1 %shard_map.37 = bf16[128,256]{1,0:T(8,128)(2,1)S(1)} custom-call(bf16[128,384]{1,0:T(8,128)(2,1)S(1)} %copy-done.1, bf16[32,320]{1,0:T(8,128)(2,1)S(1)} %copy-done.2, bf16[256,512]{1,0:T(8,128)(2,1)S(1)} %copy-done), custom_call_target="tpu_custom_call" | custom-call | tf_op jit(solution)/shard_map/pallas_call | solution.py:386
  52.7 0.6 %copy.5 = bf16[128,256]{1,0:T(8,128)(2,1)} copy(bf16[128,256]{1,0:T(8,128)(2,1)S(1)} %shard_map.37) | data formatting | bytes 131072
Async XLA Ops:
  0.0 0.9 %copy-start = (bf16[256,512]{1,0:T(8,128)(2,1)S(1)}, bf16[256,512]{1,0:T(8,128)(2,1)}, u32[]{:S(2)}) copy-start(bf16[256,512]{1,0:T(8,128)(2,1)} %w_hbm.1) | copy-start | bytes 786436
  1.0 0.9 %copy-start.1 = (bf16[128,384]{1,0:T(8,128)(2,1)S(1)}, bf16[128,384]{1,0:T(8,128)(2,1)}, u32[]{:S(2)}) copy-start(bf16[128,384]{1,0:T(8,128)(2,1)} %q_hbm.1) | copy-start | bytes 294916
  1.8 0.7 %copy-start.2 = (bf16[32,320]{1,0:T(8,128)(2,1)S(1)}, bf16[32,320]{1,0:T(8,128)(2,1)}, u32[]{:S(2)}) copy-start(bf16[32,320]{1,0:T(8,128)(2,1)} %lat_hbm.1) | copy-start | bytes 61444
